TPU v7x, 128 devices: a whole 4x4x4 slice. The times are simulated.
128 devices in a mesh: row: 8 (over x, core), col: 16 (over z, y).
Axes of the slice: x: 4, y: 4, z: 4, core: 2. Of those that a mesh axis runs over, the one named last changes fastest.
Arguments:
- kernel: bfloat16 [32768, 32768], P('row', 'col'), may hold values from -1 to 1
- random_cols: bfloat16 [32768, 256], P('row'), may hold values from -6 to 6
- tree_perm: int32 [32768], replicated, may hold values from 0 to 32767, as said below
- leaf_units: int32 [32], replicated, may hold values from 1 to 8, 160 in all
Outputs:
- bases: bfloat16 [4, 32768, 256], P(None, ('row', 'col'))
Inputs may be any that keep to these rules, and one draw needn't show every extreme that they name: `tree_perm`: A permutation. Cut tree positions and stored rows alike into blocks of 256 in order: every tree block takes at most 2 rows from any one stored block, some pair of blocks shares exactly 2, and every stored block gives 256 rows in all. `leaf_units`: they sum to 160.
All inputs are finite; a program needn't handle non-finite values.
Results may differ from a plain program's by a relative error of at most 0.0067.
Values may be sent and summed in bfloat16 or wider, within the bound.
No kernel may reach another device: no remote copies, remote signals or barrier semaphores. Data moves between devices by JAX's collectives and lax.ppermute only.
A program may use at most 192 MiB of HBM per device.

v0:
```python
import jax
import jax.numpy as jnp
from jax import lax
from jax.sharding import PartitionSpec as P

UNIT = 128
MINU = 4
LEVELS = 3


def shards(kernel, random_cols, tree_perm, leaf_units):
    width = random_cols.shape[1]
    partial_w = lax.dot_general(
        kernel, random_cols, (((0,), (0,)), ((), ())), preferred_element_type=jnp.float32
    )
    sample_w = lax.psum(partial_w, "row").astype(jnp.bfloat16)
    columns_count = lax.axis_size("col")
    rows_dev = kernel.shape[0] // columns_count
    sample = lax.psum_scatter(
        jnp.dot(kernel, sample_w, preferred_element_type=jnp.float32),
        "col",
        scatter_dimension=0,
        tiled=True,
    ).astype(jnp.bfloat16)
    total_rows = tree_perm.shape[0]
    device = lax.axis_index(("row", "col"))
    offset = device * rows_dev
    wanted = lax.dynamic_slice_in_dim(tree_perm, offset, rows_dev)
    inverse = (
        jnp.zeros((total_rows,), jnp.int32)
        .at[tree_perm]
        .set(jnp.arange(total_rows, dtype=jnp.int32))
    )
    placed = lax.dynamic_slice_in_dim(inverse, offset, rows_dev)
    everything = lax.all_gather(sample, ("row", "col"), axis=0, tiled=True)
    tree_rows = jnp.take(everything, wanted, axis=0)
    sizes = UNIT * (MINU - 1 + leaf_units)
    leaves = sizes.shape[0]
    ends = jnp.cumsum(sizes)
    positions = offset + jnp.arange(rows_dev, dtype=jnp.int32)
    leaf_of = jnp.sum(positions[:, None] >= ends[None, :], axis=1)
    reach = rows_dev // (UNIT * MINU) + 2
    offsets = jnp.arange(reach, dtype=jnp.int32)
    levels = LEVELS + 1
    node_ids = [leaf_of // 2**level for level in range(levels)]
    totals = []
    stored_leaf = jnp.sum(placed[:, None] >= ends[None, :], axis=1)
    leaf_range = jnp.arange(leaves, dtype=jnp.int32)
    chosen = stored_leaf[None, :] == leaf_range[:, None]
    masked = jnp.where(chosen[:, :, None], sample[None, :, :], jnp.zeros((), jnp.bfloat16))
    spread = jnp.einsum("lrs,rt->lst", masked, sample, preferred_element_type=jnp.float32)
    leaf_grams = lax.psum(spread, ("row", "col"))
    for level in range(levels):
        group = 2**level
        count = leaves // group
        node_grams = leaf_grams.reshape(count, group, width, width).sum(axis=1)
        index = jnp.minimum(node_ids[level][0] + offsets, count - 1)
        totals.append(jnp.take(node_grams, index, axis=0))
    identity_matrix = jnp.eye(width, dtype=jnp.float32)
    values = tree_rows.astype(jnp.float32).T
    results = []
    for level in range(levels):
        ids = node_ids[level]
        group = 2**level
        count = leaves // group
        node_sizes = sizes.reshape(count, group).sum(axis=1)
        candidate = ids[0] + offsets
        present = candidate <= ids[-1]
        counts = jnp.take(node_sizes, jnp.minimum(candidate, count - 1)).astype(jnp.float32)
        mean = jnp.where(
            present[:, None, None], totals[level] / counts[:, None, None], identity_matrix[None]
        )
        factor = jnp.linalg.cholesky(mean)
        basis = jnp.zeros((rows_dev, width), jnp.float32)
        for which in range(reach):
            solved = jax.scipy.linalg.solve_triangular(factor[which], values, lower=True).T
            basis = basis + jnp.where((ids == candidate[which])[:, None], solved, 0.0)
        results.append(basis.astype(jnp.bfloat16))
    return jnp.stack(results)


def solution(mesh):
    return jax.shard_map(
        shards,
        mesh=mesh,
        in_specs=(P("row", "col"), P("row", None), P(), P()),
        out_specs=P(None, ("row", "col"), None),
        check_vma=False,
    )
```

profile of v0, /device:TPU:1, one launch (start us, length us, event | category | flops | bytes accessed | tf_op | source)
XLA Modules:
  0.0 931.9 jit_solution(916774655061557949)
XLA Ops:
  6.5 1.6 copy-done
  8.1 9.7 %fusion.100 = f32[2048,256]{1,0:T(8,128)} fusion(bf16[4096,2048]{1,0:T(8,128)(2,1)} %param.7, bf16[4096,256]{1,0:T(8,128)(2,1)S(1)} %copy-done), kind=kOutput, calls=%fused_computation.278 | convolution fusion | flops 4294967296 | bytes 20971520 | tf_op jit(solution)/shard_map/dot_general | solution.py:13
  17.8 52.9 %all-reduce.5 = bf16[2048,256]{1,0:T(8,128)(2,1)S(1)} all-reduce(f32[2048,256]{1,0:T(8,128)} %fusion.100), channel_id=1, replica_groups=mesh['row'=8,'col'=16] {'row'}, use_global_device_ids=true, to_apply=%region_4.5 | all-reduce | flops 524288 | bytes 3145728 | tf_op jit(solution)/shard_map/psum | solution.py:16
  70.7 10.1 %convolution_bitcast_fusion = f32[4096,256]{0,1:T(8,128)} fusion(bf16[4096,2048]{1,0:T(8,128)(2,1)} %param.7, bf16[2048,256]{1,0:T(8,128)(2,1)S(1)} %all-reduce.5), kind=kOutput, calls=%fused_computation.29 | convolution fusion | flops 4294967296 | bytes 22020096 | tf_op jit(solution)/shard_map/dot_general | solution.py:20
  81.9 120.1 %scatter_custom_fusion = s32[32768]{0:T(1024)S(1)} fusion(s32[32768]{0:T(1024)S(1)} %compare_select_fusion, s32[32768]{0:T(1024)S(1)} %iota.117, s32[]{:T(128)} %copy.139), kind=kCustom, calls=%fused_computation.181 | custom fusion | bytes 131076 | tf_op jit(solution)/shard_map/scatter | solution.py:32
  203.1 4.5 fusion
  207.7 12.0 %all-gather.2.cloned.1.call-start = ((), (), s32[]{:S(2)}) async-start(), calls=%async_computation.3 | async-start | bytes 16908288 | tf_op jit(solution)/shard_map/all_gather | solution.py:35
  231.2 1.3 compare_and_fusion
  232.6 1.3 compare_and_fusion.2
  233.9 2.5 broadcast_compare_fusion.9
  236.4 2.6 broadcast_compare_fusion.11
  245.2 1.4 select_convert_fusion
  246.6 1.7 broadcast_compare_fusion.5
  248.4 1.7 broadcast_compare_fusion.8
  250.1 3.1 broadcast_compare_fusion.1
  253.2 119.0 %all-reduce.4.cloned.1.call-done = f32[32,256,256]{2,1,0:T(8,128)} async-done(((f32[32,256,256]{2,1,0:T(8,128)}), f32[32,256,256]{2,1,0:T(8,128)}) %all-reduce.4.cloned.1.call-update) | async-done | bytes 8388624 | tf_op jit(solution)/shard_map/psum | solution.py:52
  372.1 4.2 bitcast_reduce_fusion.1
  377.2 6.5 bitcast_reduce_fusion.2
  383.7 2.9 gather_fusion.3
  386.7 4.1 bitcast_reduce_fusion
  392.4 4.0 gather_fusion
  397.4 1.5 divide_select_fusion.1
  400.0 23.5 %custom-call.29 = f32[2,128,128]{2,1,0:T(8,128)S(1)} custom-call(f32[2,128,128]{2,1,0:T(8,128)S(1)} %cholesky.350), custom_call_target="Cholesky" | custom-call | tf_op jit(solution)/shard_map/jit(cholesky)/cholesky | solution.py:73
  423.7 23.5 %custom-call.39 = f32[2,128,128]{2,1,0:T(8,128)S(1)} custom-call(f32[2,128,128]{2,1,0:T(8,128)S(1)} %cholesky.356), custom_call_target="Cholesky" | custom-call | tf_op jit(solution)/shard_map/jit(cholesky)/cholesky | solution.py:73
  448.3 23.5 %custom-call.34 = f32[2,128,128]{2,1,0:T(8,128)S(1)} custom-call(f32[2,128,128]{2,1,0:T(8,128)S(1)} %cholesky.353), custom_call_target="Cholesky" | custom-call | tf_op jit(solution)/shard_map/jit(cholesky)/cholesky | solution.py:73
  472.1 23.9 %custom-call.44 = f32[2,128,128]{2,1,0:T(8,128)S(1)} custom-call(f32[2,128,128]{2,1,0:T(8,128)S(1)} %cholesky.359), custom_call_target="Cholesky" | custom-call | tf_op jit(solution)/shard_map/jit(cholesky)/cholesky | solution.py:73
  496.0 1.5 select_bitcast_fusion.1
  497.4 19.7 %custom-call.30 = f32[2,1,128,128]{2,3,1,0:T(8,128)S(1)} custom-call(f32[2,1,128,128]{3,2,1,0:T(8,128)S(1)} %get-tuple-element.180), custom_call_target="InvertDiagBlocksLowerTriangular" | custom-call | tf_op jit(solution)/shard_map/jit(cholesky)/cholesky | solution.py:73
  517.8 23.5 %custom-call.31 = f32[2,128,128]{2,1,0:T(8,128)S(1)} custom-call(f32[2,128,128]{2,1,0:T(8,128)S(1)} %convolution_subtract_fusion.11), custom_call_target="Cholesky" | custom-call | tf_op jit(solution)/shard_map/jit(cholesky)/cholesky | solution.py:73
  541.3 19.8 %custom-call.35 = f32[2,1,128,128]{2,3,1,0:T(8,128)S(1)} custom-call(f32[2,1,128,128]{3,2,1,0:T(8,128)S(1)} %get-tuple-element.178), custom_call_target="InvertDiagBlocksLowerTriangular" | custom-call | tf_op jit(solution)/shard_map/jit(cholesky)/cholesky | solution.py:73
  563.7 23.5 %custom-call.36 = f32[2,128,128]{2,1,0:T(8,128)S(1)} custom-call(f32[2,128,128]{2,1,0:T(8,128)S(1)} %convolution_subtract_fusion.10), custom_call_target="Cholesky" | custom-call | tf_op jit(solution)/shard_map/jit(cholesky)/cholesky | solution.py:73
  587.2 21.1 %custom-call.40 = f32[2,1,128,128]{2,3,1,0:T(8,128)} custom-call(f32[2,1,128,128]{3,2,1,0:T(8,128)} %get-tuple-element.177), custom_call_target="InvertDiagBlocksLowerTriangular" | custom-call | tf_op jit(solution)/shard_map/jit(cholesky)/cholesky | solution.py:73
  610.5 25.1 %custom-call.41 = f32[2,128,128]{2,1,0:T(8,128)} custom-call(f32[2,128,128]{2,1,0:T(8,128)} %convolution_subtract_fusion.9), custom_call_target="Cholesky" | custom-call | tf_op jit(solution)/shard_map/jit(cholesky)/cholesky | solution.py:73
  636.5 21.1 %custom-call.45 = f32[2,1,128,128]{2,3,1,0:T(8,128)} custom-call(f32[2,1,128,128]{3,2,1,0:T(8,128)} %get-tuple-element.179), custom_call_target="InvertDiagBlocksLowerTriangular" | custom-call | tf_op jit(solution)/shard_map/jit(cholesky)/cholesky | solution.py:73
  659.9 24.3 %custom-call.46 = f32[2,128,128]{2,1,0:T(8,128)S(1)} custom-call(f32[2,128,128]{2,1,0:T(8,128)} %convolution_subtract_fusion.8), custom_call_target="Cholesky" | custom-call | tf_op jit(solution)/shard_map/jit(cholesky)/cholesky | solution.py:73
  686.2 1.5 select_select_fusion.3
  688.4 3.8 while.23
  692.3 20.1 %custom-call.48 = f32[2,128,128]{1,2,0:T(8,128)S(1)} custom-call(f32[2,128,128]{2,1,0:T(8,128)S(1)} %get-tuple-element.64), custom_call_target="InvertDiagBlocksLowerTriangular" | custom-call | tf_op jit(solution)/shard_map/jit(_solve_triangular)/triangular_solve | solution.py:76
  712.4 4.0 while.22
  713.0 1.4 bitcast_dynamic-update-slice_fusion.22
  715.0 1.4 bitcast_dynamic-update-slice_fusion.22
  716.4 20.3 %custom-call.47 = f32[2,128,128]{1,2,0:T(8,128)} custom-call(f32[2,128,128]{2,1,0:T(8,128)S(1)} %get-tuple-element.63), custom_call_target="InvertDiagBlocksLowerTriangular" | custom-call | tf_op jit(solution)/shard_map/jit(_solve_triangular)/triangular_solve | solution.py:76
  736.7 4.1 while.21
  737.3 1.4 bitcast_dynamic-update-slice_fusion.21
  739.4 1.4 bitcast_dynamic-update-slice_fusion.21
  740.8 19.7 %custom-call.43 = f32[2,128,128]{1,2,0:T(8,128)S(1)} custom-call(f32[2,128,128]{2,1,0:T(8,128)S(1)} %get-tuple-element.62), custom_call_target="InvertDiagBlocksLowerTriangular" | custom-call | tf_op jit(solution)/shard_map/jit(_solve_triangular)/triangular_solve | solution.py:76
  760.5 3.9 while.20
  761.1 1.4 bitcast_dynamic-update-slice_fusion.20
  763.1 1.4 bitcast_dynamic-update-slice_fusion.20
  764.5 19.7 %custom-call.42 = f32[2,128,128]{1,2,0:T(8,128)S(1)} custom-call(f32[2,128,128]{2,1,0:T(8,128)S(1)} %get-tuple-element.61), custom_call_target="InvertDiagBlocksLowerTriangular" | custom-call | tf_op jit(solution)/shard_map/jit(_solve_triangular)/triangular_solve | solution.py:76
  784.2 3.9 while.19
  784.8 1.3 bitcast_dynamic-update-slice_fusion.19
  786.7 1.3 bitcast_dynamic-update-slice_fusion.19
  788.1 19.7 %custom-call.38 = f32[2,128,128]{1,2,0:T(8,128)S(1)} custom-call(f32[2,128,128]{2,1,0:T(8,128)S(1)} %get-tuple-element.60), custom_call_target="InvertDiagBlocksLowerTriangular" | custom-call | tf_op jit(solution)/shard_map/jit(_solve_triangular)/triangular_solve | solution.py:76
  807.8 4.0 while.18
  808.4 1.4 bitcast_dynamic-update-slice_fusion.18
  810.4 1.4 bitcast_dynamic-update-slice_fusion.18
  811.7 20.5 %custom-call.37 = f32[2,128,128]{1,2,0:T(8,128)} custom-call(f32[2,128,128]{2,1,0:T(8,128)S(1)} %get-tuple-element.59), custom_call_target="InvertDiagBlocksLowerTriangular" | custom-call | tf_op jit(solution)/shard_map/jit(_solve_triangular)/triangular_solve | solution.py:76
  832.3 3.8 while.17
  836.1 20.3 %custom-call.33 = f32[2,128,128]{1,2,0:T(8,128)} custom-call(f32[2,128,128]{2,1,0:T(8,128)S(1)} %get-tuple-element.58), custom_call_target="InvertDiagBlocksLowerTriangular" | custom-call | tf_op jit(solution)/shard_map/jit(_solve_triangular)/triangular_solve | solution.py:76
  856.4 3.6 while.16
  860.0 20.3 %custom-call.32 = f32[2,128,128]{1,2,0:T(8,128)} custom-call(f32[2,128,128]{2,1,0:T(8,128)S(1)} %get-tuple-element.57), custom_call_target="InvertDiagBlocksLowerTriangular" | custom-call | tf_op jit(solution)/shard_map/jit(_solve_triangular)/triangular_solve | solution.py:76
  880.3 22.6 %copy.47 = bf16[32768,256]{1,0:T(8,128)(2,1)} copy(bf16[32768,256]{0,1:T(8,128)(2,1)} %all-gather.2.cloned.1.call-done) | data formatting | bytes 33554432 | tf_op jit(solution)/shard_map/all_gather | solution.py:35
  902.9 9.0 gather_fusion.2
  (234 shorter events, 67.4 us)
Async XLA Ops:
  6.5 1.6 copy-start
  6.5 195.6 %reduce-scatter.2.cloned.1.call-start = ((), (), s32[]{:S(2)}) async-start(), calls=%async_computation.1 | async-start | bytes 4456448 | tf_op jit(solution)/shard_map/reduce_scatter | solution.py:19
  80.9 0.7 copy-start.25
  80.9 0.9 copy-start.11
  80.9 291.2 %all-reduce.4.cloned.1.call-start = ((), (), s32[]{:S(2)}) async-start(), calls=%async_computation.2 | async-start | bytes 16777216 | tf_op jit(solution)/shard_map/psum | solution.py:52
  203.1 4.5 copy-start.2
  207.7 672.6 %all-gather.2.cloned.1.call-start = ((), (), s32[]{:S(2)}) async-start(), calls=%async_computation.3 | async-start | bytes 16908288 | tf_op jit(solution)/shard_map/all_gather | solution.py:35
  399.2 0.8 copy-start.6
  423.7 93.4 %copy-start.7 = (f32[2,256,256]{2,1,0:T(8,128)S(1)}, f32[2,256,256]{2,1,0:T(8,128)}, u32[]{:S(2)}) copy-start(f32[2,256,256]{2,1,0:T(8,128)} %copy-done.6) | copy-start | bytes 1572868
  447.5 0.8 copy-start.8
  495.9 1.5 copy-start.9
  517.8 166.3 %copy-start.10 = (f32[2,128,128]{2,1,0:T(8,128)S(1)}, f32[2,128,128]{2,1,0:T(8,128)}, u32[]{:S(2)}) copy-start(f32[2,128,128]{2,1,0:T(8,128)} %copy-done.9) | copy-start | bytes 393220
  685.1 1.0 copy-start.3
  685.2 1.0 copy-start.4
  807.8 108.1 %copy-start.13 = (f32[2,128,128]{1,2,0:T(8,128)}, f32[2,128,128]{1,2,0:T(8,128)S(1)}, u32[]{:S(2)}) copy-start(f32[2,128,128]{1,2,0:T(8,128)S(1)} %custom-call.38) | copy-start | bytes 393220
  836.1 66.9 %copy-start.5 = (f32[256,256]{1,0:T(8,128)}, f32[256,256]{1,0:T(8,128)S(1)}, u32[]{:S(2)}) copy-start(f32[256,256]{1,0:T(8,128)S(1)} %get-tuple-element.602) | copy-start | bytes 786436
  880.3 31.8 %copy-start.24 = (pred[256]{0:T(512)(128)(4,1)S(1)}, pred[256]{0:T(512)(128)(4,1)}, u32[]{:S(2)}) copy-start(pred[256]{0:T(512)(128)(4,1)} %get-tuple-element.139) | copy-start | bytes 772
  880.3 32.8 %copy-start.12 = (f32[2,128,128]{1,2,0:T(8,128)S(1)}, f32[2,128,128]{1,2,0:T(8,128)}, u32[]{:S(2)}) copy-start(f32[2,128,128]{1,2,0:T(8,128)} %custom-call.47) | copy-start | bytes 393220
  912.1 10.5 %copy-start.14 = (f32[2,128,128]{1,2,0:T(8,128)S(1)}, f32[2,128,128]{1,2,0:T(8,128)}, u32[]{:S(2)}) copy-start(f32[2,128,128]{1,2,0:T(8,128)} %custom-call.33) | copy-start | bytes 393220
  912.1 10.8 %copy-start.15 = (f32[2,128,128]{1,2,0:T(8,128)S(1)}, f32[2,128,128]{1,2,0:T(8,128)}, u32[]{:S(2)}) copy-start(f32[2,128,128]{1,2,0:T(8,128)} %custom-call.32) | copy-start | bytes 393220
  912.4 11.4 %copy-start.18 = (pred[256]{0:T(512)(128)(4,1)S(1)}, pred[256]{0:T(512)(128)(4,1)}, u32[]{:S(2)}) copy-start(pred[256]{0:T(512)(128)(4,1)} %get-tuple-element.187) | copy-start | bytes 772
  912.5 11.4 %copy-start.19 = (pred[256]{0:T(512)(128)(4,1)S(1)}, pred[256]{0:T(512)(128)(4,1)}, u32[]{:S(2)}) copy-start(pred[256]{0:T(512)(128)(4,1)} %get-tuple-element.188) | copy-start | bytes 772
  913.1 10.8 %copy-start.16 = (pred[256]{0:T(512)(128)(4,1)S(1)}, pred[256]{0:T(512)(128)(4,1)}, u32[]{:S(2)}) copy-start(pred[256]{0:T(512)(128)(4,1)} %get-tuple-element.226) | copy-start | bytes 772
  913.1 10.8 %copy-start.17 = (pred[256]{0:T(512)(128)(4,1)S(1)}, pred[256]{0:T(512)(128)(4,1)}, u32[]{:S(2)}) copy-start(pred[256]{0:T(512)(128)(4,1)} %get-tuple-element.227) | copy-start | bytes 772
  913.7 10.3 %copy-start.22 = (pred[256]{0:T(512)(128)(4,1)S(1)}, pred[256]{0:T(512)(128)(4,1)}, u32[]{:S(2)}) copy-start(pred[256]{0:T(512)(128)(4,1)} %get-tuple-element.183) | copy-start | bytes 772
  913.7 10.3 %copy-start.23 = (pred[256]{0:T(512)(128)(4,1)S(1)}, pred[256]{0:T(512)(128)(4,1)}, u32[]{:S(2)}) copy-start(pred[256]{0:T(512)(128)(4,1)} %get-tuple-element.184) | copy-start | bytes 772
  914.3 9.7 %copy-start.20 = (pred[256]{0:T(512)(128)(4,1)S(1)}, pred[256]{0:T(512)(128)(4,1)}, u32[]{:S(2)}) copy-start(pred[256]{0:T(512)(128)(4,1)} %get-tuple-element.181) | copy-start | bytes 772
  914.3 9.7 %copy-start.21 = (pred[256]{0:T(512)(128)(4,1)S(1)}, pred[256]{0:T(512)(128)(4,1)}, u32[]{:S(2)}) copy-start(pred[256]{0:T(512)(128)(4,1)} %get-tuple-element.182) | copy-start | bytes 772
  916.2 9.0 copy-start.1
Sparse Core Ops, SparseCore 0:
  81.0 79.6 reduce-scatter.1
  207.8 164.3 all-reduce.3
  375.0 98.1 all-gather.1
where the time goes:
time: 940 us; the launch traced here: 932 us
  other arithmetic  481 us (51%)
  local copies, waits for them, and re-layouts  208 us (22%)
  waiting for transfers between devices  119 us (13%)
  blocking collectives  52.9 us (6%)
  matrix products  43.3 us (5%)
  between operations  14.6 us (2%)
  starting transfers between devices  12 us (1%)
    another operation x28, other arithmetic, shards(): factor = jnp.linalg.cholesky(mean)  276 us
    another operation x14, other arithmetic, shards(): jax.scipy.linalg.solve_triangular(factor[which], values, lower=True)  162 us
    scatter x1, local copies, waits for them, and re-layouts, shards(): inverse = jnp.zeros((total_rows,), jnp.int32).at[tree_perm].set(jnp.arang...  120 us
    psum x1, waiting for transfers between devices, shards(): leaf_grams = lax.psum(spread, ('row', 'col'))  119 us
    psum x1, blocking collectives, shards(): sample_w = lax.psum(partial_w, 'row').astype(jnp.bfloat16)  52.9 us
    another operation x49, local copies, waits for them, and re-layouts, shards(): jax.scipy.linalg.solve_triangular(factor[which], values, lower=True)  31.3 us
    all_gather x1, local copies, waits for them, and re-layouts, shards(): everything = lax.all_gather(sample, ('row', 'col'), axis=0, tiled=True)  22.6 us
  transfers between devices with their start and end apart: 3, of which 1 were waited for; matrix products, arithmetic and copies ran while one was open for 71% of the time, Pallas kernels for 0%

commit v1 on v0

--- a/solution.py
+++ b/solution.py
@@ -49,7 +49,9 @@
     chosen = stored_leaf[None, :] == leaf_range[:, None]
     masked = jnp.where(chosen[:, :, None], sample[None, :, :], jnp.zeros((), jnp.bfloat16))
     spread = jnp.einsum("lrs,rt->lst", masked, sample, preferred_element_type=jnp.float32)
-    leaf_grams = lax.psum(spread, ("row", "col"))
+    leaf_grams = spread
+    for m in ("row", "col"):
+        leaf_grams = lax.psum(leaf_grams, axis_name=m)
     for level in range(levels):
         group = 2**level
         count = leaves // group

time: 940 us -> 1030 us (1.096)
  waiting for transfers between devices: 119 us -> 206 us
    psum x1 -> x2, waiting for transfers between devices: 119 us -> 206 us  [shards(): leaf_grams = lax.psum(leaf_grams, axis_name=m)]
  transfers between devices with their start and end apart: 3 -> 4, of which waited for: 1 -> 2; matrix products, arithmetic and copies ran while one was open for 71% -> 65% of each run, Pallas kernels for 0% -> 0%
where the time goes in v1:
time: 1030 us; the launch traced here: 1020 us
  other arithmetic  481 us (47%)
  local copies, waits for them, and re-layouts  208 us (20%)
  waiting for transfers between devices  206 us (20%)
  blocking collectives  52.9 us (5%)
  matrix products  43.3 us (4%)
  between operations  14.6 us (1%)
  starting transfers between devices  12.1 us (1%)
    another operation x28, other arithmetic, shards(): factor = jnp.linalg.cholesky(mean)  276 us
    psum x2, waiting for transfers between devices, shards(): leaf_grams = lax.psum(leaf_grams, axis_name=m)  206 us
    another operation x14, other arithmetic, shards(): jax.scipy.linalg.solve_triangular(factor[which], values, lower=True)  162 us
    scatter x1, local copies, waits for them, and re-layouts, shards(): inverse = jnp.zeros((total_rows,), jnp.int32).at[tree_perm].set(jnp.arang...  120 us
    psum x1, blocking collectives, shards(): sample_w = lax.psum(partial_w, 'row').astype(jnp.bfloat16)  52.9 us
    another operation x49, local copies, waits for them, and re-layouts, shards(): jax.scipy.linalg.solve_triangular(factor[which], values, lower=True)  31.3 us
    all_gather x1, local copies, waits for them, and re-layouts, shards(): everything = lax.all_gather(sample, ('row', 'col'), axis=0, tiled=True)  22.6 us
  transfers between devices with their start and end apart: 4, of which 2 were waited for; matrix products, arithmetic and copies ran while one was open for 65% of the time, Pallas kernels for 0%

profile of v1, /device:TPU:1, one launch (start us, length us, event | category | flops | bytes accessed | tf_op | source)
XLA Modules:
  0.0 1019.2 jit_solution(7605801211079900988)
XLA Ops:
  6.5 1.6 copy-done
  8.1 9.7 fusion.100
  17.8 52.9 %all-reduce.8 = bf16[2048,256]{1,0:T(8,128)(2,1)S(1)} all-reduce(f32[2048,256]{1,0:T(8,128)} %fusion.100), channel_id=1, replica_groups=mesh['row'=8,'col'=16] {'row'}, use_global_device_ids=true, to_apply=%region_4.5 | all-reduce | flops 524288 | bytes 3145728 | tf_op jit(solution)/shard_map/psum | solution.py:16
  70.7 10.1 convolution_bitcast_fusion
  81.9 120.1 %scatter_custom_fusion = s32[32768]{0:T(1024)S(1)} fusion(s32[32768]{0:T(1024)S(1)} %compare_select_fusion, s32[32768]{0:T(1024)S(1)} %iota.117, s32[]{:T(128)} %copy.140), kind=kCustom, calls=%fused_computation.181 | custom fusion | bytes 131076 | tf_op jit(solution)/shard_map/scatter | solution.py:32
  203.1 4.5 fusion
  207.7 106.7 %all-reduce.5.cloned.1.call-done = f32[32,256,256]{2,1,0:T(8,128)} async-done(((f32[32,256,256]{2,1,0:T(8,128)}), f32[32,256,256]{2,1,0:T(8,128)}) %all-reduce.5.cloned.1.call-update) | async-done | bytes 8388624 | tf_op jit(solution)/shard_map/psum | solution.py:54
  314.4 12.0 %all-gather.2.cloned.1.call-start = ((), (), s32[]{:S(2)}) async-start(), calls=%async_computation.4 | async-start | bytes 16908288 | tf_op jit(solution)/shard_map/all_gather | solution.py:35
  328.3 1.3 fusion.78
  331.5 1.3 fusion.80
  338.0 1.3 compare_and_fusion
  339.3 1.3 compare_and_fusion.2
  340.6 2.6 broadcast_compare_fusion.9
  343.2 2.5 broadcast_compare_fusion.11
  353.4 1.7 broadcast_compare_fusion.5
  355.1 1.7 broadcast_compare_fusion.8
  356.8 3.1 broadcast_compare_fusion.1
  359.9 99.6 %all-reduce.7.cloned.1.call-done = f32[32,256,256]{2,1,0:T(8,128)} async-done(((f32[32,256,256]{2,1,0:T(8,128)}), f32[32,256,256]{2,1,0:T(8,128)}) %all-reduce.7.cloned.1.call-update) | async-done | bytes 8388624 | tf_op jit(solution)/shard_map/psum | solution.py:54
  459.5 4.2 bitcast_reduce_fusion.1
  464.5 6.5 bitcast_reduce_fusion.2
  471.0 2.9 gather_fusion.3
  474.1 4.1 bitcast_reduce_fusion
  479.7 4.0 gather_fusion
  484.7 1.5 divide_select_fusion.1
  487.3 23.5 %custom-call.29 = f32[2,128,128]{2,1,0:T(8,128)S(1)} custom-call(f32[2,128,128]{2,1,0:T(8,128)S(1)} %cholesky.350), custom_call_target="Cholesky" | custom-call | tf_op jit(solution)/shard_map/jit(cholesky)/cholesky | solution.py:75
  511.1 23.5 %custom-call.39 = f32[2,128,128]{2,1,0:T(8,128)S(1)} custom-call(f32[2,128,128]{2,1,0:T(8,128)S(1)} %cholesky.356), custom_call_target="Cholesky" | custom-call | tf_op jit(solution)/shard_map/jit(cholesky)/cholesky | solution.py:75
  535.6 23.5 %custom-call.34 = f32[2,128,128]{2,1,0:T(8,128)S(1)} custom-call(f32[2,128,128]{2,1,0:T(8,128)S(1)} %cholesky.353), custom_call_target="Cholesky" | custom-call | tf_op jit(solution)/shard_map/jit(cholesky)/cholesky | solution.py:75
  559.4 23.9 %custom-call.44 = f32[2,128,128]{2,1,0:T(8,128)S(1)} custom-call(f32[2,128,128]{2,1,0:T(8,128)S(1)} %cholesky.359), custom_call_target="Cholesky" | custom-call | tf_op jit(solution)/shard_map/jit(cholesky)/cholesky | solution.py:75
  583.3 1.5 select_bitcast_fusion.1
  584.8 19.7 %custom-call.30 = f32[2,1,128,128]{2,3,1,0:T(8,128)S(1)} custom-call(f32[2,1,128,128]{3,2,1,0:T(8,128)S(1)} %get-tuple-element.180), custom_call_target="InvertDiagBlocksLowerTriangular" | custom-call | tf_op jit(solution)/shard_map/jit(cholesky)/cholesky | solution.py:75
  605.1 23.5 %custom-call.31 = f32[2,128,128]{2,1,0:T(8,128)S(1)} custom-call(f32[2,128,128]{2,1,0:T(8,128)S(1)} %convolution_subtract_fusion.11), custom_call_target="Cholesky" | custom-call | tf_op jit(solution)/shard_map/jit(cholesky)/cholesky | solution.py:75
  628.6 19.8 %custom-call.35 = f32[2,1,128,128]{2,3,1,0:T(8,128)S(1)} custom-call(f32[2,1,128,128]{3,2,1,0:T(8,128)S(1)} %get-tuple-element.178), custom_call_target="InvertDiagBlocksLowerTriangular" | custom-call | tf_op jit(solution)/shard_map/jit(cholesky)/cholesky | solution.py:75
  651.0 23.5 %custom-call.36 = f32[2,128,128]{2,1,0:T(8,128)S(1)} custom-call(f32[2,128,128]{2,1,0:T(8,128)S(1)} %convolution_subtract_fusion.10), custom_call_target="Cholesky" | custom-call | tf_op jit(solution)/shard_map/jit(cholesky)/cholesky | solution.py:75
  674.5 21.1 %custom-call.40 = f32[2,1,128,128]{2,3,1,0:T(8,128)} custom-call(f32[2,1,128,128]{3,2,1,0:T(8,128)} %get-tuple-element.177), custom_call_target="InvertDiagBlocksLowerTriangular" | custom-call | tf_op jit(solution)/shard_map/jit(cholesky)/cholesky | solution.py:75
  697.8 25.1 %custom-call.41 = f32[2,128,128]{2,1,0:T(8,128)} custom-call(f32[2,128,128]{2,1,0:T(8,128)} %convolution_subtract_fusion.9), custom_call_target="Cholesky" | custom-call | tf_op jit(solution)/shard_map/jit(cholesky)/cholesky | solution.py:75
  723.8 21.1 %custom-call.45 = f32[2,1,128,128]{2,3,1,0:T(8,128)} custom-call(f32[2,1,128,128]{3,2,1,0:T(8,128)} %get-tuple-element.179), custom_call_target="InvertDiagBlocksLowerTriangular" | custom-call | tf_op jit(solution)/shard_map/jit(cholesky)/cholesky | solution.py:75
  747.2 24.3 %custom-call.46 = f32[2,128,128]{2,1,0:T(8,128)S(1)} custom-call(f32[2,128,128]{2,1,0:T(8,128)} %convolution_subtract_fusion.8), custom_call_target="Cholesky" | custom-call | tf_op jit(solution)/shard_map/jit(cholesky)/cholesky | solution.py:75
  773.5 1.5 select_select_fusion.3
  775.8 3.8 while.23
  779.6 20.1 %custom-call.48 = f32[2,128,128]{1,2,0:T(8,128)S(1)} custom-call(f32[2,128,128]{2,1,0:T(8,128)S(1)} %get-tuple-element.64), custom_call_target="InvertDiagBlocksLowerTriangular" | custom-call | tf_op jit(solution)/shard_map/jit(_solve_triangular)/triangular_solve | solution.py:78
  799.7 4.0 while.22
  800.3 1.4 bitcast_dynamic-update-slice_fusion.22
  802.3 1.4 bitcast_dynamic-update-slice_fusion.22
  803.7 20.3 %custom-call.47 = f32[2,128,128]{1,2,0:T(8,128)} custom-call(f32[2,128,128]{2,1,0:T(8,128)S(1)} %get-tuple-element.63), custom_call_target="InvertDiagBlocksLowerTriangular" | custom-call | tf_op jit(solution)/shard_map/jit(_solve_triangular)/triangular_solve | solution.py:78
  824.0 4.1 while.21
  824.6 1.4 bitcast_dynamic-update-slice_fusion.21
  826.7 1.4 bitcast_dynamic-update-slice_fusion.21
  828.1 19.7 %custom-call.43 = f32[2,128,128]{1,2,0:T(8,128)S(1)} custom-call(f32[2,128,128]{2,1,0:T(8,128)S(1)} %get-tuple-element.62), custom_call_target="InvertDiagBlocksLowerTriangular" | custom-call | tf_op jit(solution)/shard_map/jit(_solve_triangular)/triangular_solve | solution.py:78
  847.8 3.9 while.20
  848.4 1.4 bitcast_dynamic-update-slice_fusion.20
  850.4 1.4 bitcast_dynamic-update-slice_fusion.20
  851.8 19.7 %custom-call.42 = f32[2,128,128]{1,2,0:T(8,128)S(1)} custom-call(f32[2,128,128]{2,1,0:T(8,128)S(1)} %get-tuple-element.61), custom_call_target="InvertDiagBlocksLowerTriangular" | custom-call | tf_op jit(solution)/shard_map/jit(_solve_triangular)/triangular_solve | solution.py:78
  871.5 3.9 while.19
  875.4 19.7 %custom-call.38 = f32[2,128,128]{1,2,0:T(8,128)S(1)} custom-call(f32[2,128,128]{2,1,0:T(8,128)S(1)} %get-tuple-element.60), custom_call_target="InvertDiagBlocksLowerTriangular" | custom-call | tf_op jit(solution)/shard_map/jit(_solve_triangular)/triangular_solve | solution.py:78
  895.1 4.0 while.18
  895.7 1.4 bitcast_dynamic-update-slice_fusion.18
  897.7 1.4 bitcast_dynamic-update-slice_fusion.18
  899.1 20.5 %custom-call.37 = f32[2,128,128]{1,2,0:T(8,128)} custom-call(f32[2,128,128]{2,1,0:T(8,128)S(1)} %get-tuple-element.59), custom_call_target="InvertDiagBlocksLowerTriangular" | custom-call | tf_op jit(solution)/shard_map/jit(_solve_triangular)/triangular_solve | solution.py:78
  919.6 3.8 while.17
  923.4 20.3 %custom-call.33 = f32[2,128,128]{1,2,0:T(8,128)} custom-call(f32[2,128,128]{2,1,0:T(8,128)S(1)} %get-tuple-element.58), custom_call_target="InvertDiagBlocksLowerTriangular" | custom-call | tf_op jit(solution)/shard_map/jit(_solve_triangular)/triangular_solve | solution.py:78
  943.7 3.6 while.16
  947.3 20.3 %custom-call.32 = f32[2,128,128]{1,2,0:T(8,128)} custom-call(f32[2,128,128]{2,1,0:T(8,128)S(1)} %get-tuple-element.57), custom_call_target="InvertDiagBlocksLowerTriangular" | custom-call | tf_op jit(solution)/shard_map/jit(_solve_triangular)/triangular_solve | solution.py:78
  967.6 22.6 %copy.47 = bf16[32768,256]{1,0:T(8,128)(2,1)} copy(bf16[32768,256]{0,1:T(8,128)(2,1)} %all-gather.2.cloned.1.call-done) | data formatting | bytes 33554432 | tf_op jit(solution)/shard_map/all_gather | solution.py:35
  990.2 9.0 gather_fusion.2
  (237 shorter events, 68.8 us)
Async XLA Ops:
  6.5 1.6 copy-start
  6.5 195.6 %reduce-scatter.2.cloned.1.call-start = ((), (), s32[]{:S(2)}) async-start(), calls=%async_computation.1 | async-start | bytes 4456448 | tf_op jit(solution)/shard_map/reduce_scatter | solution.py:19
  80.9 0.7 copy-start.25
  80.9 0.9 copy-start.11
  80.9 233.5 %all-reduce.5.cloned.1.call-start = ((), (), s32[]{:S(2)}) async-start(), calls=%async_computation.2 | async-start | bytes 16777216 | tf_op jit(solution)/shard_map/psum | solution.py:54
  203.1 4.5 copy-start.2
  207.7 251.8 %all-reduce.7.cloned.1.call-start = ((), (), s32[]{:S(2)}) async-start(), calls=%async_computation.3 | async-start | bytes 16777216 | tf_op jit(solution)/shard_map/psum | solution.py:54
  314.4 653.2 %all-gather.2.cloned.1.call-start = ((), (), s32[]{:S(2)}) async-start(), calls=%async_computation.4 | async-start | bytes 16908288 | tf_op jit(solution)/shard_map/all_gather | solution.py:35
  486.5 0.8 copy-start.6
  511.0 93.4 %copy-start.7 = (f32[2,256,256]{2,1,0:T(8,128)S(1)}, f32[2,256,256]{2,1,0:T(8,128)}, u32[]{:S(2)}) copy-start(f32[2,256,256]{2,1,0:T(8,128)} %copy-done.6) | copy-start | bytes 1572868
  534.8 0.8 copy-start.8
  583.2 1.5 copy-start.9
  605.1 166.3 %copy-start.10 = (f32[2,128,128]{2,1,0:T(8,128)S(1)}, f32[2,128,128]{2,1,0:T(8,128)}, u32[]{:S(2)}) copy-start(f32[2,128,128]{2,1,0:T(8,128)} %copy-done.9) | copy-start | bytes 393220
  772.5 1.0 copy-start.3
  772.5 1.0 copy-start.4
  895.1 108.1 %copy-start.13 = (f32[2,128,128]{1,2,0:T(8,128)}, f32[2,128,128]{1,2,0:T(8,128)S(1)}, u32[]{:S(2)}) copy-start(f32[2,128,128]{1,2,0:T(8,128)S(1)} %custom-call.38) | copy-start | bytes 393220
  923.4 66.9 %copy-start.5 = (f32[256,256]{1,0:T(8,128)}, f32[256,256]{1,0:T(8,128)S(1)}, u32[]{:S(2)}) copy-start(f32[256,256]{1,0:T(8,128)S(1)} %get-tuple-element.606) | copy-start | bytes 786436
  967.6 31.8 %copy-start.24 = (pred[256]{0:T(512)(128)(4,1)S(1)}, pred[256]{0:T(512)(128)(4,1)}, u32[]{:S(2)}) copy-start(pred[256]{0:T(512)(128)(4,1)} %get-tuple-element.139) | copy-start | bytes 772
  967.6 32.8 %copy-start.12 = (f32[2,128,128]{1,2,0:T(8,128)S(1)}, f32[2,128,128]{1,2,0:T(8,128)}, u32[]{:S(2)}) copy-start(f32[2,128,128]{1,2,0:T(8,128)} %custom-call.47) | copy-start | bytes 393220
  999.4 10.5 %copy-start.14 = (f32[2,128,128]{1,2,0:T(8,128)S(1)}, f32[2,128,128]{1,2,0:T(8,128)}, u32[]{:S(2)}) copy-start(f32[2,128,128]{1,2,0:T(8,128)} %custom-call.33) | copy-start | bytes 393220
  999.4 10.8 %copy-start.15 = (f32[2,128,128]{1,2,0:T(8,128)S(1)}, f32[2,128,128]{1,2,0:T(8,128)}, u32[]{:S(2)}) copy-start(f32[2,128,128]{1,2,0:T(8,128)} %custom-call.32) | copy-start | bytes 393220
  999.8 11.4 %copy-start.18 = (pred[256]{0:T(512)(128)(4,1)S(1)}, pred[256]{0:T(512)(128)(4,1)}, u32[]{:S(2)}) copy-start(pred[256]{0:T(512)(128)(4,1)} %get-tuple-element.187) | copy-start | bytes 772
  999.8 11.4 %copy-start.19 = (pred[256]{0:T(512)(128)(4,1)S(1)}, pred[256]{0:T(512)(128)(4,1)}, u32[]{:S(2)}) copy-start(pred[256]{0:T(512)(128)(4,1)} %get-tuple-element.188) | copy-start | bytes 772
  1000.4 10.8 %copy-start.16 = (pred[256]{0:T(512)(128)(4,1)S(1)}, pred[256]{0:T(512)(128)(4,1)}, u32[]{:S(2)}) copy-start(pred[256]{0:T(512)(128)(4,1)} %get-tuple-element.226) | copy-start | bytes 772
  1000.4 10.8 %copy-start.17 = (pred[256]{0:T(512)(128)(4,1)S(1)}, pred[256]{0:T(512)(128)(4,1)}, u32[]{:S(2)}) copy-start(pred[256]{0:T(512)(128)(4,1)} %get-tuple-element.227) | copy-start | bytes 772
  1001.0 10.3 %copy-start.22 = (pred[256]{0:T(512)(128)(4,1)S(1)}, pred[256]{0:T(512)(128)(4,1)}, u32[]{:S(2)}) copy-start(pred[256]{0:T(512)(128)(4,1)} %get-tuple-element.183) | copy-start | bytes 772
  1001.0 10.3 %copy-start.23 = (pred[256]{0:T(512)(128)(4,1)S(1)}, pred[256]{0:T(512)(128)(4,1)}, u32[]{:S(2)}) copy-start(pred[256]{0:T(512)(128)(4,1)} %get-tuple-element.184) | copy-start | bytes 772
  1001.6 9.7 copy-start.20
  1001.6 9.7 copy-start.21
  1003.5 9.0 copy-start.1
Sparse Core Ops, SparseCore 0:
  81.0 79.6 reduce-scatter.1
  207.8 106.5 all-reduce.4
  318.0 141.4 all-reduce.6
  462.2 99.0 all-gather.1
